TPU v7x, 32 devices: a whole 2x2x4 slice. The times are simulated.
32 devices in a mesh: band: 2 (over x), tm: 16 (over z, y, core).
Axes of the slice: x: 2, y: 2, z: 4, core: 2. Of those that a mesh axis runs over, the one named last changes fastest.
Arguments:
- volts: int32 [8, 2, 3145728], P('band', None, 'tm'), parts along dimension 0, may hold values from -128 to 127, as said below
- taps: float32 [16, 4096], replicated, may hold values from -0.024 to 0.024
- pairs: int32 [4, 2], replicated, may hold values from 0 to 3, as said below
Outputs:
- coherence: float32 [8, 4096], P('band'), parts along dimension 0
- normalized: float32 [2, 8, 768, 4096], P(None, 'band', 'tm'), parts along dimension 1
There are 2 independent parts, one for each index of `band`. A program takes and returns all parts, laid end to end along the dimension named above; an argument that names none is the same for every part. Nothing has to cross between parts.
Inputs may be any that keep to these rules, and one draw needn't show every extreme that they name: `volts`: every sample is a whole number of the int8 range. Each pair names a stream of the first antenna (0 or 1) and then one of the second antenna (2 or 3); the four pairs are distinct.
All inputs are finite; a program needn't handle non-finite values.
Results may differ from a plain program's by a relative error of at most 0.000067.
Values sent between devices are 32-bit elements; how exact they have to be, the bound alone decides.
No kernel may reach another device: no remote copies, remote signals or barrier semaphores. Data moves between devices by JAX's collectives and lax.ppermute only.
A program may use at most 128 MiB of HBM per device.

v0:
```python
import functools

import jax
import jax.numpy as jnp
import numpy as np
from jax import lax
from jax.experimental import pallas as pl
from jax.experimental.pallas import tpu as pltpu
from jax.sharding import PartitionSpec as P

LANES = 128
GROUP = 8
PITCH = 40


def shifted(array, axis, by):
    devices = lax.axis_size(axis)
    pairs = [(i, i + by) for i in range(devices) if 0 <= i + by < devices]
    return lax.ppermute(array, axis, pairs)


def halves(matrix):
    matrix = np.asarray(matrix, np.float32)
    high = matrix.astype(jnp.bfloat16)
    low = (matrix - high.astype(np.float32)).astype(jnp.bfloat16)
    return high, low


@functools.lru_cache(maxsize=None)
def tables(channels):
    radix = channels // LANES
    per_row = LANES // radix
    i = np.arange(radix)
    angle = 2.0 * np.pi * ((i[:, None] * i[None, :]) % radix) / radix
    first = np.zeros((2, radix, radix, 2))
    first[0, :, :, 0] = np.cos(angle)
    first[0, :, :, 1] = np.sin(angle)
    first[1, :, :, 0] = -np.sin(angle)
    first[1, :, :, 1] = np.cos(angle)
    high, low = halves(first.reshape(2 * radix, 2 * radix))
    left = np.concatenate([high, high, low, low], axis=1)
    j = np.arange(LANES)
    twist = 2.0 * np.pi * ((i[:, None] * j[None, :]) % channels) / channels
    twist = np.stack([np.cos(twist), np.sin(twist)]).astype(np.float32)
    g = np.arange(per_row)
    s = np.arange(radix)
    b = (per_row * s[None, :] + g[:, None]).reshape(LANES)
    angle = 2.0 * np.pi * ((j[:, None] * b[None, :]) % LANES) / LANES
    cos, sin = np.cos(angle), np.sin(angle)
    second = np.block([[cos, -sin], [sin, cos]]) / np.sqrt(channels)
    high, low = halves(second)
    right = np.concatenate([high, high, low], axis=0)
    return left, twist, right


def natural(block, radix):
    turned = block.T
    per_row = LANES // radix
    return [
        jnp.concatenate(
            [turned[g * radix : (g + 1) * radix, f * radix : (f + 1) * radix] for g in range(per_row)],
            axis=1,
        )
        for f in range(per_row)
    ]


def kernel(pairs, taps, left, twist, right, acc_in, old2, old1, cur, *rest, skip, finish, aliased):
    out, sums, filt, spec, acc, nat = rest[1:] if aliased else rest
    streams = cur.shape[0]
    count = pairs.shape[0]
    n_taps, rows, _ = taps.shape
    radix = rows // 2
    step = pl.program_id(0)
    last = pl.num_programs(0) - 1
    per_row = LANES // radix
    behind1 = GROUP
    behind2 = n_taps - 1 - GROUP
    tiles = rows // 8

    @pl.when(step == 0)
    def _():
        acc[...] = acc_in[...]

    def filter_tile(index, carry):
        s = index // tiles
        q = pl.multiple_of((index % tiles) * 8, 8)
        coef = [taps[t, pl.ds(q, 8), :] for t in range(n_taps)]
        total = [None] * GROUP
        for w in range(n_taps - 1 + GROUP):
            if w < behind2:
                x = old2[s, pl.ds((w + skip) * rows + q, 8), :]
            elif w < behind2 + behind1:
                x = old1[s, pl.ds((w - behind2) * rows + q, 8), :]
            else:
                x = cur[s, pl.ds((w - behind2 - behind1) * rows + q, 8), :]
            x = x.astype(jnp.float32)
            for m in range(GROUP):
                t = m + n_taps - 1 - w
                if 0 <= t < n_taps:
                    term = coef[t] * x
                    total[m] = term if total[m] is None else total[m] + term
        for m in range(GROUP):
            filt[s, pl.ds(m * rows + q, 8), :] = total[m]
        return carry

    lax.fori_loop(0, streams * tiles, filter_tile, 0)

    def transform(s, carry):
        turned = []
        for pair in range(GROUP // 2):
            columns = []
            for f in (2 * pair, 2 * pair + 1):
                x = filt[s, f * rows : (f + 1) * rows, :]
                high = x.astype(jnp.bfloat16)
                low = (x - high.astype(jnp.float32)).astype(jnp.bfloat16)
                columns.append(jnp.concatenate([high, low, high, low], axis=0))
            y = jnp.dot(
                left[...], jnp.concatenate(columns, axis=1), preferred_element_type=jnp.float32
            )
            for f in range(2):
                re = y[:radix, f * LANES : (f + 1) * LANES]
                im = y[radix:, f * LANES : (f + 1) * LANES]
                z = jnp.concatenate(
                    [re * twist[0] + im * twist[1], im * twist[0] - re * twist[1]], axis=1
                )
                turned.append(z)
        z = jnp.concatenate(turned, axis=0)
        high = z.astype(jnp.bfloat16)
        low = (z - high.astype(jnp.float32)).astype(jnp.bfloat16)
        full = jnp.dot(
            jnp.concatenate([high, low, high], axis=1),
            right[...],
            preferred_element_type=jnp.float32,
        )
        spec[s] = full
        power = full[:, :LANES] * full[:, :LANES] + full[:, LANES:] * full[:, LANES:]
        acc[s] += power.reshape(GROUP, radix, LANES).sum(axis=0)
        return carry

    lax.fori_loop(0, streams, transform, 0)

    def correlate(p, carry):
        a = pairs[p, 0]
        b = pairs[p, 1]
        for half in range(GROUP // per_row):
            span = slice(half * LANES, (half + 1) * LANES)
            a_re = spec[a, span, :LANES]
            a_im = spec[a, span, LANES:]
            b_re = spec[b, span, :LANES]
            b_im = spec[b, span, LANES:]
            for part in range(2):
                if part == 0:
                    prod = a_re * b_re + a_im * b_im
                else:
                    prod = a_im * b_re - a_re * b_im
                acc[streams + part * count + p] += prod.reshape(per_row, radix, LANES).sum(axis=0)
                for f, block in enumerate(natural(prod, radix)):
                    start = (half * per_row + f) * PITCH
                    nat[part, start : start + radix, :] = block
        for part in range(2):
            for s in range(radix):
                out[part, p, :, s * LANES : (s + 1) * LANES] = nat[
                    part, pl.ds(s, GROUP, stride=PITCH), :
                ]
        return carry

    lax.fori_loop(0, count, correlate, 0)

    @pl.when(step == last)
    def _():
        if finish:
            for first in range(0, streams + 2 * count, per_row):
                block = acc[first : first + per_row].reshape(LANES, LANES)
                for f, piece in enumerate(natural(block, radix)):
                    sums[first + f] = piece
        else:
            sums[...] = acc[...]


def channelize(consts, acc_in, old2, old1, cur, base, steps, skip, finish, spectra, shape):
    streams = cur[0].shape[0]
    rows = consts[1].shape[1]
    radix = rows // 2
    size = GROUP * rows

    def block(entry):
        array, first = entry
        return pl.BlockSpec(
            (streams, min(size, array.shape[1]), LANES), lambda i: (0, first + i, 0)
        )

    whole = pl.BlockSpec(memory_space=pltpu.VMEM)
    ins = [pl.BlockSpec(memory_space=pltpu.SMEM)] + [whole] * 5
    ins += [block(old2), block(old1), block(cur)]
    args = list(consts) + [acc_in, old2[0], old1[0], cur[0]]
    aliases = {}
    if spectra is not None:
        ins.append(pl.BlockSpec(memory_space=pl.ANY))
        args.append(spectra)
        aliases = {len(args) - 1: 0}
    parts, count, frames, channels = shape
    return pl.pallas_call(
        functools.partial(kernel, skip=skip, finish=finish, aliased=spectra is not None),
        grid=(steps,),
        in_specs=ins,
        out_specs=[
            pl.BlockSpec((parts, count, GROUP, channels), lambda i: (0, 0, base + i, 0)),
            whole,
        ],
        out_shape=[
            jax.ShapeDtypeStruct(shape, jnp.float32),
            jax.ShapeDtypeStruct(acc_in.shape, jnp.float32),
        ],
        scratch_shapes=[
            pltpu.VMEM((streams, size, LANES), jnp.float32),
            pltpu.VMEM((streams, GROUP * radix, 2 * LANES), jnp.float32),
            pltpu.VMEM(acc_in.shape, jnp.float32),
            pltpu.VMEM((2, GROUP * PITCH, LANES), jnp.float32),
        ],
        input_output_aliases=aliases,
        compiler_params=pltpu.CompilerParams(vmem_limit_bytes=40 << 20),
        name="channelize",
    )(*args)


def scale_kernel(factor, prod, out):
    for p in range(prod.shape[1]):
        out[:, p] = prod[:, p] * factor[p : p + 1, :][None]


def rescale(products, factor):
    parts, count, frames, channels = products.shape
    spec = pl.BlockSpec((parts, count, GROUP, channels), lambda i: (0, 0, i, 0))
    return pl.pallas_call(
        scale_kernel,
        grid=(frames // GROUP,),
        in_specs=[pl.BlockSpec(memory_space=pltpu.VMEM), spec],
        out_specs=spec,
        out_shape=jax.ShapeDtypeStruct(products.shape, jnp.float32),
        input_output_aliases={1: 0},
        name="rescale",
    )(factor, products)


def on_device(volts, taps, pairs):
    streams, comps, local = volts.shape
    n_taps, channels = taps.shape
    count = pairs.shape[0]
    edge = n_taps - 1
    frames = local // channels
    radix = channels // LANES
    rows = comps * radix
    devices = lax.axis_size("tm")
    samples = volts.reshape(streams, comps, local // LANES, LANES)
    samples = samples.transpose(0, 2, 1, 3).reshape(streams, frames * rows, LANES)
    near = shifted(samples[:, (frames - GROUP) * rows :], "tm", 1)
    far = shifted(samples[:, (frames - edge) * rows : (frames - GROUP) * rows], "tm", 1)
    left, twist, right = tables(channels)
    coef = jnp.repeat(taps.reshape(n_taps, radix, LANES), comps, axis=1)
    consts = (pairs, coef, jnp.asarray(left), jnp.asarray(twist), jnp.asarray(right))
    acc = jnp.zeros((streams + 2 * count, radix, LANES), jnp.float32)
    shape = (2, count, frames, channels)
    rest = frames // GROUP - 2
    spectra, acc = channelize(
        consts, acc, (samples, 0), (samples, 1), (samples, 2), 2, rest, 1, False, None, shape
    )
    spectra, acc = channelize(
        consts, acc, (near, 0), (samples, 0), (samples, 1), 1, 1, 1, False, spectra, shape
    )
    spectra, acc = channelize(
        consts, acc, (far, 0), (near, 0), (samples, 0), 0, 1, 0, True, spectra, shape
    )
    sums = acc.reshape(streams + 2 * count, devices, channels // devices)
    sums = lax.all_to_all(sums.transpose(1, 0, 2), "tm", 0, 0)
    mean = jnp.sum(sums, axis=0) / (frames * devices)
    auto = mean[:streams] + 1e-06
    cross_re = mean[streams : streams + count]
    cross_im = mean[streams + count :]
    denom = jnp.take(auto, pairs[:, 0], axis=0) * jnp.take(auto, pairs[:, 1], axis=0)
    coherence = (cross_re * cross_re + cross_im * cross_im) / denom
    factor = 1.0 / jnp.sqrt(denom)
    both = lax.all_gather(jnp.concatenate([coherence, factor]), "tm", axis=0)
    both = both.transpose(1, 0, 2).reshape(2 * count, channels)
    return (both[:count], rescale(spectra, both[count:]))


def solution(mesh):
    return jax.shard_map(
        on_device,
        mesh=mesh,
        in_specs=(P("band", None, "tm"), P(), P()),
        out_specs=(P("band", None), P(None, "band", "tm", None)),
        check_vma=False,
    )
```

profile of v0, /device:TPU:0, one launch (start us, length us, event | category | flops | bytes accessed | tf_op | source)
XLA Modules:
  0.0 102.2 jit_solution(17875703840186574103)
XLA Ops:
  0.6 0.0 slice-start
  0.6 2.4 %slice.48 = s32[4,512,128]{2,1,0:T(8,128)} slice(s32[4,3072,128]{2,1,0:T(8,128)} %bitcast.27), slice={[0:4], [2560:3072], [0:128]} | slice | bytes 2097152 | tf_op jit(solution)/shard_map/slice | solution.py:257
  3.1 2.5 %collective-permute-start = (s32[4,512,128]{2,1,0:T(8,128)}, s32[4,512,128]{2,1,0:T(8,128)S(1)}, u32[]{:S(2)}, u32[]{:S(2)}) collective-permute-start(s32[4,512,128]{2,1,0:T(8,128)} %slice.48), channel_id=1, source_target_pairs={{0,1},{1,2},{2,3},{3,4},{4,5},{5,6},{6,7},{7,8},{8,9},{9,10},{10,1... | collective-permute-start | bytes 3145736 | tf_op jit(solution)/shard_map/ppermute | solution.py:19
  5.5 2.2 %slice.49 = s32[4,448,128]{2,1,0:T(8,128)} slice(s32[4,3072,128]{2,1,0:T(8,128)} %bitcast.28), slice={[0:4], [2112:2560], [0:128]} | slice | bytes 1835008 | tf_op jit(solution)/shard_map/slice | solution.py:258
  7.7 5.4 %collective-permute-start.1 = (s32[4,448,128]{2,1,0:T(8,128)}, s32[4,448,128]{2,1,0:T(8,128)}, u32[]{:S(2)}, u32[]{:S(2)}) collective-permute-start(s32[4,448,128]{2,1,0:T(8,128)} %slice.49), channel_id=1, source_target_pairs={{0,1},{1,2},{2,3},{3,4},{4,5},{5,6},{6,7},{7,8},{8,9},{9,10},{10,1... | collective-permute-start | bytes 2752520 | tf_op jit(solution)/shard_map/ppermute | solution.py:19
  13.1 1.0 copy.22
  14.1 0.8 copy.19.pairs
  14.9 0.2 broadcast_in_dim.15
  15.1 0.0 copy-start
  15.1 2.8 %copy-done = s32[4,2,196608]{2,1,0:T(2,128)S(1)} copy-done((s32[4,2,196608]{2,1,0:T(2,128)S(1)}, s32[4,2,196608]{2,1,0:T(2,128)}, u32[]{:S(2)}) %copy-start) | copy-done | bytes 6291480
  17.9 0.0 copy-start.1
  17.9 1.0 copy-done.1
  18.9 0.0 copy-start.2
  18.9 0.8 copy-done.2
  19.7 0.0 copy-start.3
  19.7 0.8 copy-done.3
  20.4 0.0 slice-start.1
  20.4 23.6 %channelize.3 = (f32[2,4,48,4096]{3,2,1,0:T(8,128)}, f32[12,32,128]{2,1,0:T(8,128)S(1)}) custom-call(s32[4,2]{1,0:T(4,128)S(1)} %copy.19.pairs, f32[16,64,128]{2,1,0:T(8,128)S(1)} %bitcast.37, bf16[64,256]{1,0:T(8,128)(2,1)S(1)} %copy-done.2, f32[2,32,128]{2,1,0:T(8,128)S(1)} %copy-done.3, bf16[768,256]{1,0:T(8,128)(2,1)S(1)} %copy-done.1, ...), custom_call_target="tpu_custom_call" | custom-call | tf_op jit(solution)/shard_map/channelize/pallas_call | solution.py:203
  44.1 0.0 collective-permute-done.old2.old1
  44.1 0.0 slice-done
  44.1 0.0 slice-done.1
  44.1 6.9 %channelize.4 = (f32[2,4,48,4096]{3,2,1,0:T(8,128)}, f32[12,32,128]{2,1,0:T(8,128)S(1)}) custom-call(s32[4,2]{1,0:T(4,128)S(1)} %copy.19.pairs, f32[16,64,128]{2,1,0:T(8,128)S(1)} %bitcast.38, bf16[64,256]{1,0:T(8,128)(2,1)S(1)} %copy-done.2, f32[2,32,128]{2,1,0:T(8,128)S(1)} %copy-done.3, ...), custom_call_target="tpu_custom_call", output_to_operand_aliasing={{0}: (9, {})} | custom-call | tf_op jit(solution)/shard_map/channelize/pallas_call | solution.py:203
  50.9 0.0 collective-permute-done.1.old2
  50.9 0.0 copy-start.4
  51.0 7.7 %channelize.5 = (f32[2,4,48,4096]{3,2,1,0:T(8,128)}, f32[12,32,128]{2,1,0:T(8,128)S(1)}) custom-call(s32[4,2]{1,0:T(4,128)S(1)} %copy.19.pairs, f32[16,64,128]{2,1,0:T(8,128)S(1)} %bitcast.39, bf16[64,256]{1,0:T(8,128)(2,1)S(1)} %copy-done.2, f32[2,32,128]{2,1,0:T(8,128)S(1)} %copy-done.3, ...), custom_call_target="tpu_custom_call", output_to_operand_aliasing={{0}: (9, {})} | custom-call | tf_op jit(solution)/shard_map/channelize/pallas_call | solution.py:203
  58.7 0.1 reshape.31
  58.8 0.8 copy.27
  59.6 4.1 %all-to-all-start = ((f32[16,12,256]{2,1,0:T(8,128)}), f32[16,12,256]{2,1,0:T(8,128)S(1)}, u32[]{:S(2)}, u32[]{:S(2)}) async-start(f32[16,12,256]{2,1,0:T(8,128)} %bitcast.25), calls=%async_computation | async-start | bytes 524288 | tf_op jit(solution)/shard_map/all_to_all | solution.py:275
  63.6 0.0 copy-done.4
  63.7 10.0 %all-to-all-done = f32[16,12,256]{2,1,0:T(8,128)S(1)} async-done(((f32[16,12,256]{2,1,0:T(8,128)}), f32[16,12,256]{2,1,0:T(8,128)S(1)}, u32[]{:S(2)}, u32[]{:S(2)}) %all-to-all-start) | async-done | bytes 196640 | tf_op jit(solution)/shard_map/all_to_all | solution.py:275
  73.7 0.6 gather_fusion
  74.3 0.6 gather_fusion.1
  74.8 0.1 fusion.1
  74.9 18.9 %all-gather = f32[128,256]{1,0:T(8,128)S(1)} all-gather(f32[8,256]{1,0:T(8,128)S(1)} %pad_maximum_fusion), channel_id=2, replica_groups=mesh['band'=2,'tm'=16] {'tm'}, dimensions={0}, use_global_device_ids=true | all-gather | bytes 139264 | tf_op jit(solution)/shard_map/all_gather | solution.py:283
  93.9 0.7 copy.24
  94.6 0.7 copy.23
  95.3 6.9 %rescale.1 = f32[2,4,48,4096]{3,2,1,0:T(8,128)} custom-call(f32[4,4096]{1,0:T(4,128)} %bitcast.43, f32[2,4,48,4096]{3,2,1,0:T(8,128)} %get-tuple-element.14.prod), custom_call_target="tpu_custom_call", output_to_operand_aliasing={{}: (1, {})} | custom-call | tf_op jit(solution)/shard_map/rescale/pallas_call | solution.py:235
  (10 shorter events, 0.1 us)
Async XLA Ops:
  0.6 43.4 %slice-start = ((s8[6291456]{0:T(1024)(128)(4,1)}), s8[2097152]{0:T(1024)(128)(4,1)S(1)}, s32[]{:S(2)}) async-start(s8[6291456]{0:T(1024)(128)(4,1)} %bitcast.32), calls=%async_computation.1 | async-start | bytes 4194304
  3.1 41.0 %collective-permute-start = (s32[4,512,128]{2,1,0:T(8,128)}, s32[4,512,128]{2,1,0:T(8,128)S(1)}, u32[]{:S(2)}, u32[]{:S(2)}) collective-permute-start(s32[4,512,128]{2,1,0:T(8,128)} %slice.48), channel_id=1, source_target_pairs={{0,1},{1,2},{2,3},{3,4},{4,5},{5,6},{6,7},{7,8},{8,9},{9,10},{10,1... | collective-permute-start | bytes 3145736 | tf_op jit(solution)/shard_map/ppermute | solution.py:19
  7.7 43.2 %collective-permute-start.1 = (s32[4,448,128]{2,1,0:T(8,128)}, s32[4,448,128]{2,1,0:T(8,128)}, u32[]{:S(2)}, u32[]{:S(2)}) collective-permute-start(s32[4,448,128]{2,1,0:T(8,128)} %slice.49), channel_id=1, source_target_pairs={{0,1},{1,2},{2,3},{3,4},{4,5},{5,6},{6,7},{7,8},{8,9},{9,10},{10,1... | collective-permute-start | bytes 2752520 | tf_op jit(solution)/shard_map/ppermute | solution.py:19
  15.1 2.8 %copy-start = (s32[4,2,196608]{2,1,0:T(2,128)S(1)}, s32[4,2,196608]{2,1,0:T(2,128)}, u32[]{:S(2)}) copy-start(s32[4,2,196608]{2,1,0:T(2,128)} %param.8) | copy-start | bytes 18874372
  17.9 1.0 copy-start.1
  18.9 0.8 copy-start.2
  19.7 0.8 copy-start.3
  20.4 23.6 %slice-start.1 = ((s8[6291456]{0:T(1024)(128)(4,1)}), s8[4194304]{0:T(1024)(128)(4,1)S(1)}, s32[]{:S(2)}) async-start(s8[6291456]{0:T(1024)(128)(4,1)} %bitcast.32), calls=%async_computation.2 | async-start | bytes 8388608
  50.9 12.7 %copy-start.4 = (s32[4,2]{0,1:T(2,128)S(1)}, s32[4,2]{0,1:T(2,128)}, u32[]{:S(2)}) copy-start(s32[4,2]{0,1:T(2,128)} %param.10) | copy-start | bytes 100
  59.6 14.1 %all-to-all-start = ((f32[16,12,256]{2,1,0:T(8,128)}), f32[16,12,256]{2,1,0:T(8,128)S(1)}, u32[]{:S(2)}, u32[]{:S(2)}) async-start(f32[16,12,256]{2,1,0:T(8,128)} %bitcast.25), calls=%async_computation | async-start | bytes 524288 | tf_op jit(solution)/shard_map/all_to_all | solution.py:275
where the time goes:
time: 103 us; the launch traced here: 102 us
  Pallas kernels  45.1 us (44%)
  blocking collectives  18.9 us (18%)
  local copies, waits for them, and re-layouts  15.3 us (15%)
  starting transfers between devices  11.9 us (12%)
  waiting for transfers between devices  9.98 us (10%)
    pallas_call x3, Pallas kernels, channelize(): pl.pallas_call(functools.partial(kernel, skip=skip, finish=finish, aliase...  38.2 us
    all_gather x1, blocking collectives, on_device(): both = lax.all_gather(jnp.concatenate([coherence, factor]), 'tm', axis=0)  18.9 us
    all_to_all x1, waiting for transfers between devices, on_device(): sums = lax.all_to_all(sums.transpose(1, 0, 2), 'tm', 0, 0)  9.97 us
    unnamed x19, local copies, waits for them, and re-layouts  8.43 us
    ppermute x2, starting transfers between devices, shifted(): return lax.ppermute(array, axis, pairs)  7.85 us
    pallas_call x1, Pallas kernels, rescale(): pl.pallas_call(scale_kernel, grid=(frames // GROUP,), in_specs=[pl.BlockS...  6.89 us
    all_to_all x1, starting transfers between devices, on_device(): sums = lax.all_to_all(sums.transpose(1, 0, 2), 'tm', 0, 0)  4.05 us
    slice x1, local copies, waits for them, and re-layouts, on_device(): near = shifted(samples[:, (frames - GROUP) * rows:], 'tm', 1)  2.43 us
  transfers between devices with their start and end apart: 3, of which 1 were waited for; matrix products, arithmetic and copies ran while one was open for 4% of the time, Pallas kernels for 30%

commit v1 on v0

--- a/solution.py
+++ b/solution.py
@@ -65,8 +65,34 @@
     ]
 
 
-def kernel(pairs, taps, left, twist, right, acc_in, old2, old1, cur, *rest, skip, finish, aliased):
-    out, sums, filt, spec, acc, nat = rest[1:] if aliased else rest
+def cut_kernel(block2, block1, far, near):
+    far[...] = block2[:, block2.shape[1] - far.shape[1] :, :]
+    near[...] = block1[...]
+
+
+def cut(samples, rows, edge):
+    streams, total, lanes = samples.shape
+    size = GROUP * rows
+    blocks = total // size
+    whole = pl.BlockSpec(memory_space=pltpu.VMEM)
+    return pl.pallas_call(
+        cut_kernel,
+        grid=(1,),
+        in_specs=[
+            pl.BlockSpec((streams, size, lanes), lambda i: (0, blocks - 2, 0)),
+            pl.BlockSpec((streams, size, lanes), lambda i: (0, blocks - 1, 0)),
+        ],
+        out_specs=[whole, whole],
+        out_shape=[
+            jax.ShapeDtypeStruct((streams, (edge - GROUP) * rows, lanes), samples.dtype),
+            jax.ShapeDtypeStruct((streams, size, lanes), samples.dtype),
+        ],
+        compiler_params=pltpu.CompilerParams(vmem_limit_bytes=58 << 20),
+        name="cut",
+    )(samples, samples)
+
+
+def kernel(pairs, taps, left, twist, right, acc_in, old2, old1, cur, spec, sums, filt, acc, *, skip, finish):
     streams = cur.shape[0]
     count = pairs.shape[0]
     n_taps, rows, _ = taps.shape
@@ -143,26 +169,18 @@
     def correlate(p, carry):
         a = pairs[p, 0]
         b = pairs[p, 1]
-        for half in range(GROUP // per_row):
-            span = slice(half * LANES, (half + 1) * LANES)
+        total_re = acc[streams + p]
+        total_im = acc[streams + count + p]
+        for f in range(GROUP):
+            span = slice(f * radix, (f + 1) * radix)
             a_re = spec[a, span, :LANES]
             a_im = spec[a, span, LANES:]
             b_re = spec[b, span, :LANES]
             b_im = spec[b, span, LANES:]
-            for part in range(2):
-                if part == 0:
-                    prod = a_re * b_re + a_im * b_im
-                else:
-                    prod = a_im * b_re - a_re * b_im
-                acc[streams + part * count + p] += prod.reshape(per_row, radix, LANES).sum(axis=0)
-                for f, block in enumerate(natural(prod, radix)):
-                    start = (half * per_row + f) * PITCH
-                    nat[part, start : start + radix, :] = block
-        for part in range(2):
-            for s in range(radix):
-                out[part, p, :, s * LANES : (s + 1) * LANES] = nat[
-                    part, pl.ds(s, GROUP, stride=PITCH), :
-                ]
+            total_re = total_re + (a_re * b_re + a_im * b_im)
+            total_im = total_im + (a_im * b_re - a_re * b_im)
+        acc[streams + p] = total_re
+        acc[streams + count + p] = total_im
         return carry
 
     lax.fori_loop(0, count, correlate, 0)
@@ -178,7 +196,7 @@
             sums[...] = acc[...]
 
 
-def channelize(consts, acc_in, old2, old1, cur, base, steps, skip, finish, spectra, shape):
+def channelize(consts, acc_in, old2, old1, cur, steps, skip, finish):
     streams = cur[0].shape[0]
     rows = consts[1].shape[1]
     radix = rows // 2
@@ -194,53 +212,151 @@
     ins = [pl.BlockSpec(memory_space=pltpu.SMEM)] + [whole] * 5
     ins += [block(old2), block(old1), block(cur)]
     args = list(consts) + [acc_in, old2[0], old1[0], cur[0]]
-    aliases = {}
-    if spectra is not None:
-        ins.append(pl.BlockSpec(memory_space=pl.ANY))
-        args.append(spectra)
-        aliases = {len(args) - 1: 0}
-    parts, count, frames, channels = shape
     return pl.pallas_call(
-        functools.partial(kernel, skip=skip, finish=finish, aliased=spectra is not None),
+        functools.partial(kernel, skip=skip, finish=finish),
         grid=(steps,),
         in_specs=ins,
         out_specs=[
-            pl.BlockSpec((parts, count, GROUP, channels), lambda i: (0, 0, base + i, 0)),
+            pl.BlockSpec((streams, GROUP * radix, 2 * LANES), lambda i: (0, i, 0)),
             whole,
         ],
         out_shape=[
-            jax.ShapeDtypeStruct(shape, jnp.float32),
+            jax.ShapeDtypeStruct((streams, steps * GROUP * radix, 2 * LANES), jnp.float32),
             jax.ShapeDtypeStruct(acc_in.shape, jnp.float32),
         ],
         scratch_shapes=[
             pltpu.VMEM((streams, size, LANES), jnp.float32),
-            pltpu.VMEM((streams, GROUP * radix, 2 * LANES), jnp.float32),
             pltpu.VMEM(acc_in.shape, jnp.float32),
-            pltpu.VMEM((2, GROUP * PITCH, LANES), jnp.float32),
-        ],
-        input_output_aliases=aliases,
-        compiler_params=pltpu.CompilerParams(vmem_limit_bytes=40 << 20),
+        ],
+        compiler_params=pltpu.CompilerParams(vmem_limit_bytes=58 << 20),
         name="channelize",
     )(*args)
 
 
-def scale_kernel(factor, prod, out):
-    for p in range(prod.shape[1]):
-        out[:, p] = prod[:, p] * factor[p : p + 1, :][None]
-
-
-def rescale(products, factor):
-    parts, count, frames, channels = products.shape
-    spec = pl.BlockSpec((parts, count, GROUP, channels), lambda i: (0, 0, i, 0))
+def multiply_kernel(pairs, *refs):
+    *specs, out, nat = refs
+    count = pairs.shape[0]
+    radix = out.shape[3] // LANES
+    per_row = LANES // radix
+
+    def work(spec):
+        def correlate(p, carry):
+            a = pairs[p, 0]
+            b = pairs[p, 1]
+            for half in range(GROUP // per_row):
+                span = slice(half * LANES, (half + 1) * LANES)
+                a_re = spec[a, span, :LANES]
+                a_im = spec[a, span, LANES:]
+                b_re = spec[b, span, :LANES]
+                b_im = spec[b, span, LANES:]
+                for part in range(2):
+                    if part == 0:
+                        prod = a_re * b_re + a_im * b_im
+                    else:
+                        prod = a_im * b_re - a_re * b_im
+                    for f, block in enumerate(natural(prod, radix)):
+                        start = (half * per_row + f) * PITCH
+                        nat[part, start : start + radix, :] = block
+            for part in range(2):
+                for s in range(radix):
+                    out[part, p, :, s * LANES : (s + 1) * LANES] = nat[
+                        part, pl.ds(s, GROUP, stride=PITCH), :
+                    ]
+            return carry
+
+        lax.fori_loop(0, count, correlate, 0)
+
+    if len(specs) == 1:
+        work(specs[0])
+    else:
+        for index, spec in enumerate(specs):
+            pl.when(pl.program_id(0) == index)(functools.partial(work, spec))
+
+
+def multiply(pairs, specs, channels):
+    streams = specs[0].shape[0]
+    radix = channels // LANES
+    size = GROUP * radix
+    count = pairs.shape[0]
+    if len(specs) == 1:
+        steps = specs[0].shape[1] // size
+        ins = [pl.BlockSpec((streams, size, 2 * LANES), lambda i: (0, i, 0))]
+    else:
+        steps = len(specs)
+        ins = [pl.BlockSpec((streams, size, 2 * LANES), lambda i: (0, 0, 0))] * steps
+    return pl.pallas_call(
+        multiply_kernel,
+        grid=(steps,),
+        in_specs=[pl.BlockSpec(memory_space=pltpu.SMEM)] + ins,
+        out_specs=pl.BlockSpec((2, count, GROUP, channels), lambda i: (0, 0, i, 0)),
+        out_shape=jax.ShapeDtypeStruct((2, count, steps * GROUP, channels), jnp.float32),
+        scratch_shapes=[pltpu.VMEM((2, GROUP * PITCH, LANES), jnp.float32)],
+        compiler_params=pltpu.CompilerParams(vmem_limit_bytes=58 << 20),
+        name="multiply",
+    )(pairs, *specs)
+
+
+def finish_kernel(pairs, sums, out, auto, *, frames):
+    count = pairs.shape[0]
+    streams = sums.shape[1] - 2 * count
+    mean = jnp.sum(sums[...], axis=0) / frames
+    auto[...] = mean[:streams] + 1e-06
+    for p in range(count):
+        a = auto[pl.ds(pairs[p, 0], 1), :]
+        b = auto[pl.ds(pairs[p, 1], 1), :]
+        denom = a * b
+        re = mean[streams + p : streams + p + 1]
+        im = mean[streams + count + p : streams + count + p + 1]
+        coherence = (re * re + im * im) / denom
+        factor = 1.0 / jnp.sqrt(denom)
+        for d in range(out.shape[0]):
+            out[d, p : p + 1, :] = coherence
+            out[d, count + p : count + p + 1, :] = factor
+
+
+def finish_sums(pairs, sums, frames):
+    devices, lines, width = sums.shape
+    count = pairs.shape[0]
+    whole = pl.BlockSpec(memory_space=pltpu.VMEM)
+    return pl.pallas_call(
+        functools.partial(finish_kernel, frames=frames),
+        in_specs=[pl.BlockSpec(memory_space=pltpu.SMEM), whole],
+        out_specs=whole,
+        out_shape=jax.ShapeDtypeStruct((devices, 2 * count, width), jnp.float32),
+        scratch_shapes=[pltpu.VMEM((lines - 2 * count, width), jnp.float32)],
+        compiler_params=pltpu.CompilerParams(vmem_limit_bytes=12 << 20),
+        name="finish",
+    )(pairs, sums)
+
+
+def scale_kernel(factor, early, late, out):
+    step = pl.program_id(0)
+
+    def scale(prod):
+        for p in range(prod.shape[1]):
+            out[:, p] = prod[:, p] * factor[p : p + 1, :][None]
+
+    pl.when(step < 2)(functools.partial(scale, early))
+    pl.when(step >= 2)(functools.partial(scale, late))
+
+
+def rescale(early, late, factor):
+    parts, count, frames, channels = late.shape
+    block = (parts, count, GROUP, channels)
+    total = frames + early.shape[2]
     return pl.pallas_call(
         scale_kernel,
-        grid=(frames // GROUP,),
-        in_specs=[pl.BlockSpec(memory_space=pltpu.VMEM), spec],
-        out_specs=spec,
-        out_shape=jax.ShapeDtypeStruct(products.shape, jnp.float32),
-        input_output_aliases={1: 0},
+        grid=(total // GROUP,),
+        in_specs=[
+            pl.BlockSpec(memory_space=pltpu.VMEM),
+            pl.BlockSpec(block, lambda i: (0, 0, jnp.minimum(i, 1), 0)),
+            pl.BlockSpec(block, lambda i: (0, 0, jnp.maximum(i - 2, 0), 0)),
+        ],
+        out_specs=pl.BlockSpec(block, lambda i: (0, 0, i, 0)),
+        out_shape=jax.ShapeDtypeStruct((parts, count, total, channels), jnp.float32),
+        compiler_params=pltpu.CompilerParams(vmem_limit_bytes=58 << 20),
         name="rescale",
-    )(factor, products)
+    )(factor, early, late)
 
 
 def on_device(volts, taps, pairs):
@@ -254,35 +370,24 @@
     devices = lax.axis_size("tm")
     samples = volts.reshape(streams, comps, local // LANES, LANES)
     samples = samples.transpose(0, 2, 1, 3).reshape(streams, frames * rows, LANES)
-    near = shifted(samples[:, (frames - GROUP) * rows :], "tm", 1)
-    far = shifted(samples[:, (frames - edge) * rows : (frames - GROUP) * rows], "tm", 1)
+    far, near = cut(samples, rows, edge)
+    near = shifted(near, "tm", 1)
+    far = shifted(far, "tm", 1)
     left, twist, right = tables(channels)
     coef = jnp.repeat(taps.reshape(n_taps, radix, LANES), comps, axis=1)
     consts = (pairs, coef, jnp.asarray(left), jnp.asarray(twist), jnp.asarray(right))
     acc = jnp.zeros((streams + 2 * count, radix, LANES), jnp.float32)
-    shape = (2, count, frames, channels)
     rest = frames // GROUP - 2
-    spectra, acc = channelize(
-        consts, acc, (samples, 0), (samples, 1), (samples, 2), 2, rest, 1, False, None, shape
-    )
-    spectra, acc = channelize(
-        consts, acc, (near, 0), (samples, 0), (samples, 1), 1, 1, 1, False, spectra, shape
-    )
-    spectra, acc = channelize(
-        consts, acc, (far, 0), (near, 0), (samples, 0), 0, 1, 0, True, spectra, shape
-    )
+    spec2, acc = channelize(consts, acc, (samples, 0), (samples, 1), (samples, 2), rest, 1, False)
+    spec1, acc = channelize(consts, acc, (near, 0), (samples, 0), (samples, 1), 1, 1, False)
+    spec0, acc = channelize(consts, acc, (far, 0), (near, 0), (samples, 0), 1, 0, True)
     sums = acc.reshape(streams + 2 * count, devices, channels // devices)
     sums = lax.all_to_all(sums.transpose(1, 0, 2), "tm", 0, 0)
-    mean = jnp.sum(sums, axis=0) / (frames * devices)
-    auto = mean[:streams] + 1e-06
-    cross_re = mean[streams : streams + count]
-    cross_im = mean[streams + count :]
-    denom = jnp.take(auto, pairs[:, 0], axis=0) * jnp.take(auto, pairs[:, 1], axis=0)
-    coherence = (cross_re * cross_re + cross_im * cross_im) / denom
-    factor = 1.0 / jnp.sqrt(denom)
-    both = lax.all_gather(jnp.concatenate([coherence, factor]), "tm", axis=0)
+    late = multiply(pairs, [spec2], channels)
+    both = lax.all_to_all(finish_sums(pairs, sums, frames * devices), "tm", 0, 0)
+    early = multiply(pairs, [spec0, spec1], channels)
     both = both.transpose(1, 0, 2).reshape(2 * count, channels)
-    return (both[:count], rescale(spectra, both[count:]))
+    return (both[:count], rescale(early, late, both[count:]))
 
 
 def solution(mesh):

time: 103 us -> 92.5 us (0.90)
  Pallas kernels: 45.1 us -> 59.9 us
  waiting for transfers between devices: 9.98 us -> 0.01 us
  local copies, waits for them, and re-layouts: 15.3 us -> 6.11 us
  blocking collectives: 18.9 us -> 14.7 us
  starting transfers between devices: 11.9 us -> 10.5 us
    all_gather x1 -> x0, blocking collectives: 18.9 us -> none  [on_device(): both = lax.all_gather(jnp.concatenate([coherence, factor]), 'tm', axis=0)]
    all_to_all x0 -> x1, blocking collectives: none -> 14.7 us  [on_device(): sums = lax.all_to_all(sums.transpose(1, 0, 2), 'tm', 0, 0)]
    pallas_call x4 -> x8, Pallas kernels: 45.1 us -> 59.9 us  [the longest x3 33.3 us: channelize(): pl.pallas_call(functools.partial(kernel, skip=skip, finish=finish), grid=...]
    all_to_all x1, waiting for transfers between devices: 9.97 us -> 0.01 us  [on_device(): lax.all_to_all(finish_sums(pairs, sums, frames * devices), 'tm', 0, 0)]
    unnamed x19 -> x12, local copies, waits for them, and re-layouts: 8.43 us -> 2.66 us
    slice x2 -> x1, local copies, waits for them, and re-layouts: 4.64 us -> 0.66 us  [on_device(): return (both[:count], rescale(early, late, both[count:]))]
    gather x2 -> x0, local copies, waits for them, and re-layouts: 1.12 us -> none  [the longest x1 0.56 us: on_device(): jnp.take(auto, pairs[:, 0], axis=0) * jnp.take(auto, pairs[:, 1], axis=0)]
  transfers between devices with their start and end apart: 3 -> 3, of which waited for: 1 -> 0; matrix products, arithmetic and copies ran while one was open for 4% -> 3% of each run, Pallas kernels for 30% -> 45%
where the time goes in v1:
time: 92.5 us; the launch traced here: 91.9 us
  Pallas kernels  59.9 us (65%)
  blocking collectives  14.7 us (16%)
  starting transfers between devices  10.5 us (11%)
  local copies, waits for them, and re-layouts  6.11 us (7%)
    pallas_call x3, Pallas kernels, channelize(): pl.pallas_call(functools.partial(kernel, skip=skip, finish=finish), grid=...  33.3 us
    pallas_call x2, Pallas kernels, multiply(): pl.pallas_call(multiply_kernel, grid=(steps,), in_specs=[pl.BlockSpec(mem...  15 us
    all_to_all x1, blocking collectives, on_device(): sums = lax.all_to_all(sums.transpose(1, 0, 2), 'tm', 0, 0)  14.7 us
    pallas_call x1, Pallas kernels, rescale(): pl.pallas_call(scale_kernel, grid=(total // GROUP,), in_specs=[pl.BlockSp...  7.4 us
    ppermute x2, starting transfers between devices, shifted(): return lax.ppermute(array, axis, pairs)  6.97 us
    all_to_all x1, starting transfers between devices, on_device(): lax.all_to_all(finish_sums(pairs, sums, frames * devices), 'tm', 0, 0)  3.51 us
    pallas_call x1, Pallas kernels, cut(): pl.pallas_call(cut_kernel, grid=(1,), in_specs=[pl.BlockSpec((streams, si...  2.92 us
    unnamed x12, local copies, waits for them, and re-layouts  2.66 us
  transfers between devices with their start and end apart: 3, of which 0 were waited for; matrix products, arithmetic and copies ran while one was open for 3% of the time, Pallas kernels for 45%

profile of v1, /device:TPU:0, one launch (start us, length us, event | category | flops | bytes accessed | tf_op | source)
XLA Modules:
  0.0 91.9 jit_solution(160544151912808277)
XLA Ops:
  0.6 0.0 copy-start.4
  0.6 0.0 copy-start.3
  0.6 2.9 %cut.1 = (s32[4,448,128]{2,1,0:T(8,128)}, s32[4,512,128]{2,1,0:T(8,128)}) custom-call(s32[4,3072,128]{2,1,0:T(8,128)} %bitcast.14, s32[4,3072,128]{2,1,0:T(8,128)} %bitcast.15), custom_call_target="tpu_custom_call" | custom-call | tf_op jit(solution)/shard_map/cut/pallas_call | solution.py:78
  3.6 2.5 %collective-permute-start = (s32[4,512,128]{2,1,0:T(8,128)}, s32[4,512,128]{2,1,0:T(8,128)S(1)}, u32[]{:S(2)}, u32[]{:S(2)}) collective-permute-start(s32[4,512,128]{2,1,0:T(8,128)} %get-tuple-element.11), channel_id=1, source_target_pairs={{0,1},{1,2},{2,3},{3,4},{4,5},{5,6},{6,7},{7,8},{8,9},{9,10},{10,1... | collective-permute-start | bytes 3145736 | tf_op jit(solution)/shard_map/ppermute | solution.py:19
  6.0 4.5 %collective-permute-start.1 = (s32[4,448,128]{2,1,0:T(8,128)}, s32[4,448,128]{2,1,0:T(8,128)S(1)}, u32[]{:S(2)}, u32[]{:S(2)}) collective-permute-start(s32[4,448,128]{2,1,0:T(8,128)} %get-tuple-element.13), channel_id=1, source_target_pairs={{0,1},{1,2},{2,3},{3,4},{4,5},{5,6},{6,7},{7,8},{8,9},{9,10},{10,1... | collective-permute-start | bytes 2752520 | tf_op jit(solution)/shard_map/ppermute | solution.py:19
  10.6 0.0 copy-done.4
  10.6 0.7 copy.20.pairs
  11.2 0.0 copy-done.3
  11.2 0.1 copy.23
  11.3 1.0 %broadcast_in_dim.6 = f32[16,32,2,128]{3,2,1,0:T(2,128)} broadcast(f32[16,32,128]{2,1,0:T(8,128)S(1)} %bitcast.25), dimensions={0,1,3} | broadcast | bytes 786432 | tf_op jit(solution)/shard_map/broadcast_in_dim | solution.py:377
  12.3 0.7 broadcast_in_dim.7.acc_in
  13.0 19.0 %channelize.3 = (f32[4,1024,256]{2,1,0:T(8,128)}, f32[12,32,128]{2,1,0:T(8,128)}) custom-call(s32[4,2]{1,0:T(4,128)} %copy.20.pairs, f32[16,64,128]{2,1,0:T(8,128)} %bitcast.22, bf16[64,256]{1,0:T(8,128)(2,1)} %constant.8.clone.left, f32[2,32,128]{2,1,0:T(8,128)} %constant.9.clone.twist, bf16[768,256]{1,0:T(8,128)(2,1)} %constant.10.clone.right, ...), custom_call_target="tpu_custom_call" | custom-call | tf_op jit(solution)/shard_map/channelize/pallas_call | solution.py:215
  31.9 0.0 collective-permute-done.old2.old1
  31.9 0.0 copy-start.1
  32.0 1.0 %copy-done.1 = s32[4,512,128]{2,1,0:T(8,128)} copy-done((s32[4,512,128]{2,1,0:T(8,128)}, s32[4,512,128]{2,1,0:T(8,128)S(1)}, u32[]{:S(2)}) %copy-start.1) | copy-done | bytes 1048600
  32.9 7.2 %channelize.4 = (f32[4,256,256]{2,1,0:T(8,128)}, f32[12,32,128]{2,1,0:T(8,128)}) custom-call(s32[4,2]{1,0:T(4,128)} %copy.20.pairs, f32[16,64,128]{2,1,0:T(8,128)} %bitcast.23, bf16[64,256]{1,0:T(8,128)(2,1)} %constant.8.clone.left, f32[2,32,128]{2,1,0:T(8,128)} %constant.9.clone.twist, bf16[768,256]{1,0:T(8,128)(2,1)} %constant.10.clone.right, ...), custom_call_target="tpu_custom_call" | custom-call | tf_op jit(solution)/shard_map/channelize/pallas_call | solution.py:215
  40.1 0.0 collective-permute-done.1.old2
  40.1 0.0 copy-start.2
  40.1 1.0 %copy-done.2 = s32[4,448,128]{2,1,0:T(8,128)} copy-done((s32[4,448,128]{2,1,0:T(8,128)}, s32[4,448,128]{2,1,0:T(8,128)S(1)}, u32[]{:S(2)}) %copy-start.2) | copy-done | bytes 917528
  41.1 0.0 copy-start
  41.1 7.2 %channelize.5 = (f32[4,256,256]{2,1,0:T(8,128)}, f32[12,32,128]{2,1,0:T(8,128)}) custom-call(s32[4,2]{1,0:T(4,128)} %copy.20.pairs, f32[16,64,128]{2,1,0:T(8,128)} %bitcast.24, bf16[64,256]{1,0:T(8,128)(2,1)} %constant.8.clone.left, f32[2,32,128]{2,1,0:T(8,128)} %constant.9.clone.twist, bf16[768,256]{1,0:T(8,128)(2,1)} %constant.10.clone.right, ...), custom_call_target="tpu_custom_call" | custom-call | tf_op jit(solution)/shard_map/channelize/pallas_call | solution.py:215
  48.2 1.0 %reshape.26 = f32[12,16,256]{2,1,0:T(8,128)S(1)} reshape(f32[12,32,128]{2,1,0:T(8,128)} %get-tuple-element.14) | data formatting | bytes 393216 | tf_op jit(solution)/shard_map/reshape | solution.py:384
  49.2 0.1 copy.25
  49.3 14.7 %all_to_all.10.sums = f32[16,12,256]{2,1,0:T(8,128)S(1)} all-to-all(f32[16,12,256]{2,1,0:T(8,128)S(1)} %bitcast.26), channel_id=1, replica_groups=mesh['band'=2,'tm'=16] {'tm'}, dimensions={0} | all-to-all | bytes 393216 | tf_op jit(solution)/shard_map/all_to_all | solution.py:385
  64.1 0.0 copy-done
  64.1 1.3 %finish.1 = f32[16,8,256]{2,1,0:T(8,128)} custom-call(s32[4,2]{1,0:T(4,128)S(1)} %copy-done, f32[16,12,256]{2,1,0:T(8,128)S(1)} %all_to_all.10.sums), custom_call_target="tpu_custom_call" | custom-call | tf_op jit(solution)/shard_map/finish/pallas_call | solution.py:321
  65.4 3.5 %all-to-all-start.1 = ((f32[16,8,256]{2,1,0:T(8,128)}), f32[16,8,256]{2,1,0:T(8,128)S(1)}, u32[]{:S(2)}, u32[]{:S(2)}) async-start(f32[16,8,256]{2,1,0:T(8,128)} %finish.1), calls=%async_computation.1 | async-start | bytes 262144 | tf_op jit(solution)/shard_map/all_to_all | solution.py:387
  68.9 9.0 %multiply.3.late = f32[2,4,32,4096]{3,2,1,0:T(8,128)} custom-call(s32[4,2]{1,0:T(4,128)} %copy.20.pairs, f32[4,1024,256]{2,1,0:T(8,128)} %get-tuple-element.17.refs_0_), custom_call_target="tpu_custom_call" | custom-call | tf_op jit(solution)/shard_map/multiply/pallas_call | solution.py:287
  77.9 6.0 %multiply.2.early = f32[2,4,16,4096]{3,2,1,0:T(8,128)} custom-call(s32[4,2]{1,0:T(4,128)} %copy.20.pairs, f32[4,256,256]{2,1,0:T(8,128)} %get-tuple-element.15.refs_0_, f32[4,256,256]{2,1,0:T(8,128)} %get-tuple-element.16.refs_1_), custom_call_target="tpu_custom_call" | custom-call | tf_op jit(solution)/shard_map/multiply/pallas_call | solution.py:287
  83.9 0.0 all-to-all-done.1
  83.9 0.7 fusion
  84.5 7.4 %rescale.1 = f32[2,4,48,4096]{3,2,1,0:T(8,128)} custom-call(f32[4,4096]{1,0:T(4,128)} %bitcast.28, f32[2,4,16,4096]{3,2,1,0:T(8,128)} %multiply.2.early, f32[2,4,32,4096]{3,2,1,0:T(8,128)} %multiply.3.late), custom_call_target="tpu_custom_call" | custom-call | tf_op jit(solution)/shard_map/rescale/pallas_call | solution.py:347
Async XLA Ops:
  0.6 9.9 %copy-start.4 = (s32[4,2]{0,1:T(2,128)S(1)}, s32[4,2]{0,1:T(2,128)}, u32[]{:S(2)}) copy-start(s32[4,2]{0,1:T(2,128)} %param.8) | copy-start | bytes 100
  0.6 10.6 %copy-start.3 = (f32[16,4096]{1,0:T(8,128)S(1)}, f32[16,4096]{1,0:T(8,128)}, u32[]{:S(2)}) copy-start(f32[16,4096]{1,0:T(8,128)} %param.7) | copy-start | bytes 786436
  3.6 28.4 %collective-permute-start = (s32[4,512,128]{2,1,0:T(8,128)}, s32[4,512,128]{2,1,0:T(8,128)S(1)}, u32[]{:S(2)}, u32[]{:S(2)}) collective-permute-start(s32[4,512,128]{2,1,0:T(8,128)} %get-tuple-element.11), channel_id=1, source_target_pairs={{0,1},{1,2},{2,3},{3,4},{4,5},{5,6},{6,7},{7,8},{8,9},{9,10},{10,1... | collective-permute-start | bytes 3145736 | tf_op jit(solution)/shard_map/ppermute | solution.py:19
  6.0 34.0 %collective-permute-start.1 = (s32[4,448,128]{2,1,0:T(8,128)}, s32[4,448,128]{2,1,0:T(8,128)S(1)}, u32[]{:S(2)}, u32[]{:S(2)}) collective-permute-start(s32[4,448,128]{2,1,0:T(8,128)} %get-tuple-element.13), channel_id=1, source_target_pairs={{0,1},{1,2},{2,3},{3,4},{4,5},{5,6},{6,7},{7,8},{8,9},{9,10},{10,1... | collective-permute-start | bytes 2752520 | tf_op jit(solution)/shard_map/ppermute | solution.py:19
  31.9 1.0 %copy-start.1 = (s32[4,512,128]{2,1,0:T(8,128)}, s32[4,512,128]{2,1,0:T(8,128)S(1)}, u32[]{:S(2)}) copy-start(s32[4,512,128]{2,1,0:T(8,128)S(1)} %collective-permute-done.old2.old1) | copy-start | bytes 3145732
  40.1 1.0 %copy-start.2 = (s32[4,448,128]{2,1,0:T(8,128)}, s32[4,448,128]{2,1,0:T(8,128)S(1)}, u32[]{:S(2)}) copy-start(s32[4,448,128]{2,1,0:T(8,128)S(1)} %collective-permute-done.1.old2) | copy-start | bytes 2752516
  41.1 23.0 %copy-start = (s32[4,2]{1,0:T(4,128)S(1)}, s32[4,2]{1,0:T(4,128)}, u32[]{:S(2)}) copy-start(s32[4,2]{1,0:T(4,128)} %copy.20.pairs) | copy-start | bytes 100
  65.4 18.5 %all-to-all-start.1 = ((f32[16,8,256]{2,1,0:T(8,128)}), f32[16,8,256]{2,1,0:T(8,128)S(1)}, u32[]{:S(2)}, u32[]{:S(2)}) async-start(f32[16,8,256]{2,1,0:T(8,128)} %finish.1), calls=%async_computation.1 | async-start | bytes 262144 | tf_op jit(solution)/shard_map/all_to_all | solution.py:387

commit v2 on v1

--- a/solution.py
+++ b/solution.py
@@ -65,9 +65,11 @@
     ]
 
 
-def cut_kernel(block2, block1, far, near):
-    far[...] = block2[:, block2.shape[1] - far.shape[1] :, :]
-    near[...] = block1[...]
+def cut_kernel(block2, block1, out):
+    size = block1.shape[1]
+    early = out.shape[1] - size
+    out[:, :early, :] = block2[:, size - early :, :]
+    out[:, early:, :] = block1[...]
 
 
 def cut(samples, rows, edge):
@@ -82,44 +84,44 @@
             pl.BlockSpec((streams, size, lanes), lambda i: (0, blocks - 2, 0)),
             pl.BlockSpec((streams, size, lanes), lambda i: (0, blocks - 1, 0)),
         ],
-        out_specs=[whole, whole],
-        out_shape=[
-            jax.ShapeDtypeStruct((streams, (edge - GROUP) * rows, lanes), samples.dtype),
-            jax.ShapeDtypeStruct((streams, size, lanes), samples.dtype),
-        ],
+        out_specs=whole,
+        out_shape=jax.ShapeDtypeStruct((streams, edge * rows, lanes), samples.dtype),
         compiler_params=pltpu.CompilerParams(vmem_limit_bytes=58 << 20),
         name="cut",
     )(samples, samples)
 
 
-def kernel(pairs, taps, left, twist, right, acc_in, old2, old1, cur, spec, sums, filt, acc, *, skip, finish):
-    streams = cur.shape[0]
+def kernel(pairs, taps, left, twist, right, acc_in, *rest, head):
+    *sources, spec, sums, filt, acc = rest
+    streams = sources[0].shape[0]
     count = pairs.shape[0]
     n_taps, rows, _ = taps.shape
     radix = rows // 2
     step = pl.program_id(0)
     last = pl.num_programs(0) - 1
     per_row = LANES // radix
-    behind1 = GROUP
-    behind2 = n_taps - 1 - GROUP
+    edge = n_taps - 1
     tiles = rows // 8
+
+    def place(w, index):
+        if head:
+            at = w + index * GROUP
+            return (sources[0], at) if at < edge else (sources[1], at - edge)
+        at = w + 2 * GROUP - edge
+        return sources[at // GROUP], at % GROUP
 
     @pl.when(step == 0)
     def _():
         acc[...] = acc_in[...]
 
-    def filter_tile(index, carry):
+    def filter_tile(index, carry, which):
         s = index // tiles
         q = pl.multiple_of((index % tiles) * 8, 8)
         coef = [taps[t, pl.ds(q, 8), :] for t in range(n_taps)]
         total = [None] * GROUP
         for w in range(n_taps - 1 + GROUP):
-            if w < behind2:
-                x = old2[s, pl.ds((w + skip) * rows + q, 8), :]
-            elif w < behind2 + behind1:
-                x = old1[s, pl.ds((w - behind2) * rows + q, 8), :]
-            else:
-                x = cur[s, pl.ds((w - behind2 - behind1) * rows + q, 8), :]
+            ref, frame = place(w, which)
+            x = ref[s, pl.ds(frame * rows + q, 8), :]
             x = x.astype(jnp.float32)
             for m in range(GROUP):
                 t = m + n_taps - 1 - w
@@ -130,7 +132,14 @@
             filt[s, pl.ds(m * rows + q, 8), :] = total[m]
         return carry
 
-    lax.fori_loop(0, streams * tiles, filter_tile, 0)
+    def filter_all(which):
+        lax.fori_loop(0, streams * tiles, functools.partial(filter_tile, which=which), 0)
+
+    if head:
+        for which in range(2):
+            pl.when(step == which)(functools.partial(filter_all, which))
+    else:
+        filter_all(0)
 
     def transform(s, carry):
         turned = []
@@ -187,7 +196,7 @@
 
     @pl.when(step == last)
     def _():
-        if finish:
+        if head:
             for first in range(0, streams + 2 * count, per_row):
                 block = acc[first : first + per_row].reshape(LANES, LANES)
                 for f, piece in enumerate(natural(block, radix)):
@@ -196,24 +205,31 @@
             sums[...] = acc[...]
 
 
-def channelize(consts, acc_in, old2, old1, cur, steps, skip, finish):
-    streams = cur[0].shape[0]
+def channelize(consts, acc_in, samples, halo):
+    streams, total, _ = samples.shape
     rows = consts[1].shape[1]
     radix = rows // 2
     size = GROUP * rows
-
-    def block(entry):
-        array, first = entry
-        return pl.BlockSpec(
-            (streams, min(size, array.shape[1]), LANES), lambda i: (0, first + i, 0)
-        )
-
     whole = pl.BlockSpec(memory_space=pltpu.VMEM)
     ins = [pl.BlockSpec(memory_space=pltpu.SMEM)] + [whole] * 5
-    ins += [block(old2), block(old1), block(cur)]
-    args = list(consts) + [acc_in, old2[0], old1[0], cur[0]]
-    return pl.pallas_call(
-        functools.partial(kernel, skip=skip, finish=finish),
+    args = list(consts) + [acc_in]
+    head = halo is not None
+    if head:
+        steps = 2
+        ins += [
+            pl.BlockSpec(halo.shape, lambda i: (0, 0, 0)),
+            pl.BlockSpec((streams, 2 * size, LANES), lambda i: (0, 0, 0)),
+        ]
+        args += [halo, samples]
+    else:
+        steps = total // size - 2
+        for shift in range(3):
+            ins.append(
+                pl.BlockSpec((streams, size, LANES), functools.partial(lambda d, i: (0, i + d, 0), shift))
+            )
+            args.append(samples)
+    return pl.pallas_call(
+        functools.partial(kernel, head=head),
         grid=(steps,),
         in_specs=ins,
         out_specs=[
@@ -233,57 +249,44 @@
     )(*args)
 
 
-def multiply_kernel(pairs, *refs):
-    *specs, out, nat = refs
+def multiply_kernel(pairs, spec, out, nat):
     count = pairs.shape[0]
     radix = out.shape[3] // LANES
     per_row = LANES // radix
 
-    def work(spec):
-        def correlate(p, carry):
-            a = pairs[p, 0]
-            b = pairs[p, 1]
-            for half in range(GROUP // per_row):
-                span = slice(half * LANES, (half + 1) * LANES)
-                a_re = spec[a, span, :LANES]
-                a_im = spec[a, span, LANES:]
-                b_re = spec[b, span, :LANES]
-                b_im = spec[b, span, LANES:]
-                for part in range(2):
-                    if part == 0:
-                        prod = a_re * b_re + a_im * b_im
-                    else:
-                        prod = a_im * b_re - a_re * b_im
-                    for f, block in enumerate(natural(prod, radix)):
-                        start = (half * per_row + f) * PITCH
-                        nat[part, start : start + radix, :] = block
+    def correlate(p, carry):
+        a = pairs[p, 0]
+        b = pairs[p, 1]
+        for half in range(GROUP // per_row):
+            span = slice(half * LANES, (half + 1) * LANES)
+            a_re = spec[a, span, :LANES]
+            a_im = spec[a, span, LANES:]
+            b_re = spec[b, span, :LANES]
+            b_im = spec[b, span, LANES:]
             for part in range(2):
-                for s in range(radix):
-                    out[part, p, :, s * LANES : (s + 1) * LANES] = nat[
-                        part, pl.ds(s, GROUP, stride=PITCH), :
-                    ]
-            return carry
-
-        lax.fori_loop(0, count, correlate, 0)
-
-    if len(specs) == 1:
-        work(specs[0])
-    else:
-        for index, spec in enumerate(specs):
-            pl.when(pl.program_id(0) == index)(functools.partial(work, spec))
-
-
-def multiply(pairs, specs, channels):
-    streams = specs[0].shape[0]
-    radix = channels // LANES
-    size = GROUP * radix
-    count = pairs.shape[0]
-    if len(specs) == 1:
-        steps = specs[0].shape[1] // size
-        ins = [pl.BlockSpec((streams, size, 2 * LANES), lambda i: (0, i, 0))]
-    else:
-        steps = len(specs)
-        ins = [pl.BlockSpec((streams, size, 2 * LANES), lambda i: (0, 0, 0))] * steps
+                if part == 0:
+                    prod = a_re * b_re + a_im * b_im
+                else:
+                    prod = a_im * b_re - a_re * b_im
+                for f, block in enumerate(natural(prod, radix)):
+                    start = (half * per_row + f) * PITCH
+                    nat[part, start : start + radix, :] = block
+        for part in range(2):
+            for s in range(radix):
+                out[part, p, :, s * LANES : (s + 1) * LANES] = nat[
+                    part, pl.ds(s, GROUP, stride=PITCH), :
+                ]
+        return carry
+
+    lax.fori_loop(0, count, correlate, 0)
+
+
+def multiply(pairs, spectra, channels):
+    streams = spectra.shape[0]
+    size = GROUP * (channels // LANES)
+    count = pairs.shape[0]
+    steps = spectra.shape[1] // size
+    ins = [pl.BlockSpec((streams, size, 2 * LANES), lambda i: (0, i, 0))]
     return pl.pallas_call(
         multiply_kernel,
         grid=(steps,),
@@ -293,10 +296,10 @@
         scratch_shapes=[pltpu.VMEM((2, GROUP * PITCH, LANES), jnp.float32)],
         compiler_params=pltpu.CompilerParams(vmem_limit_bytes=58 << 20),
         name="multiply",
-    )(pairs, *specs)
-
-
-def finish_kernel(pairs, sums, out, auto, *, frames):
+    )(pairs, spectra)
+
+
+def finish_kernel(pairs, sums, after, out, auto, *, frames):
     count = pairs.shape[0]
     streams = sums.shape[1] - 2 * count
     mean = jnp.sum(sums[...], axis=0) / frames
@@ -314,19 +317,19 @@
             out[d, count + p : count + p + 1, :] = factor
 
 
-def finish_sums(pairs, sums, frames):
+def finish_sums(pairs, sums, after, frames):
     devices, lines, width = sums.shape
     count = pairs.shape[0]
     whole = pl.BlockSpec(memory_space=pltpu.VMEM)
     return pl.pallas_call(
         functools.partial(finish_kernel, frames=frames),
-        in_specs=[pl.BlockSpec(memory_space=pltpu.SMEM), whole],
+        in_specs=[pl.BlockSpec(memory_space=pltpu.SMEM), whole, pl.BlockSpec(memory_space=pltpu.HBM)],
         out_specs=whole,
         out_shape=jax.ShapeDtypeStruct((devices, 2 * count, width), jnp.float32),
         scratch_shapes=[pltpu.VMEM((lines - 2 * count, width), jnp.float32)],
         compiler_params=pltpu.CompilerParams(vmem_limit_bytes=12 << 20),
         name="finish",
-    )(pairs, sums)
+    )(pairs, sums, after)
 
 
 def scale_kernel(factor, early, late, out):
@@ -370,22 +373,18 @@
     devices = lax.axis_size("tm")
     samples = volts.reshape(streams, comps, local // LANES, LANES)
     samples = samples.transpose(0, 2, 1, 3).reshape(streams, frames * rows, LANES)
-    far, near = cut(samples, rows, edge)
-    near = shifted(near, "tm", 1)
-    far = shifted(far, "tm", 1)
+    halo = shifted(cut(samples, rows, edge), "tm", 1)
     left, twist, right = tables(channels)
     coef = jnp.repeat(taps.reshape(n_taps, radix, LANES), comps, axis=1)
     consts = (pairs, coef, jnp.asarray(left), jnp.asarray(twist), jnp.asarray(right))
     acc = jnp.zeros((streams + 2 * count, radix, LANES), jnp.float32)
-    rest = frames // GROUP - 2
-    spec2, acc = channelize(consts, acc, (samples, 0), (samples, 1), (samples, 2), rest, 1, False)
-    spec1, acc = channelize(consts, acc, (near, 0), (samples, 0), (samples, 1), 1, 1, False)
-    spec0, acc = channelize(consts, acc, (far, 0), (near, 0), (samples, 0), 1, 0, True)
+    spec_late, acc = channelize(consts, acc, samples, None)
+    spec_early, acc = channelize(consts, acc, samples, halo)
     sums = acc.reshape(streams + 2 * count, devices, channels // devices)
     sums = lax.all_to_all(sums.transpose(1, 0, 2), "tm", 0, 0)
-    late = multiply(pairs, [spec2], channels)
-    both = lax.all_to_all(finish_sums(pairs, sums, frames * devices), "tm", 0, 0)
-    early = multiply(pairs, [spec0, spec1], channels)
+    late = multiply(pairs, spec_late, channels)
+    both = lax.all_to_all(finish_sums(pairs, sums, late[0, 0, :GROUP, :LANES], frames * devices), "tm", 0, 0)
+    early = multiply(pairs, spec_early, channels)
     both = both.transpose(1, 0, 2).reshape(2 * count, channels)
     return (both[:count], rescale(early, late, both[count:]))
 

time: 92.5 us -> 85.6 us (0.925)
  blocking collectives: 14.7 us -> 0 us
  starting transfers between devices: 10.5 us -> 17.8 us
  Pallas kernels: 59.9 us -> 57 us
  waiting for transfers between devices: 0.01 us -> 2.61 us
    all_to_all x1 -> x0, blocking collectives: 14.7 us -> none  [on_device(): sums = lax.all_to_all(sums.transpose(1, 0, 2), 'tm', 0, 0)]
    all_to_all x1 -> x2, starting transfers between devices: 3.51 us -> 15.3 us  [the longest x1 9.65 us: on_device(): sums = lax.all_to_all(sums.transpose(1, 0, 2), 'tm', 0, 0)]
    ppermute x2 -> x1, starting transfers between devices: 6.97 us -> 2.51 us  [shifted(): return lax.ppermute(array, axis, pairs)]
    all_to_all x1 -> x2, waiting for transfers between devices: 0.01 us -> 2.61 us  [the longest x1 2.28 us: on_device(): lax.all_to_all(finish_sums(pairs, sums, late[0, 0, :GROUP, :LANES], frame...]
    pallas_call x3 -> x2, Pallas kernels: 33.3 us -> 30.7 us  [channelize(): pl.pallas_call(functools.partial(kernel, head=head), grid=(steps,), in_sp...]
    unnamed x12 -> x10, local copies, waits for them, and re-layouts: 2.66 us -> 2.02 us
  transfers between devices with their start and end apart: 3 -> 3, of which waited for: 0 -> 2; matrix products, arithmetic and copies ran while one was open for 3% -> 4% of each run, Pallas kernels for 45% -> 40%
where the time goes in v2:
time: 85.6 us; the launch traced here: 85 us
  Pallas kernels  57 us (67%)
  starting transfers between devices  17.8 us (21%)
  local copies, waits for them, and re-layouts  6.83 us (8%)
  waiting for transfers between devices  2.61 us (3%)
    pallas_call x2, Pallas kernels, channelize(): pl.pallas_call(functools.partial(kernel, head=head), grid=(steps,), in_sp...  30.7 us
    pallas_call x2, Pallas kernels, multiply(): pl.pallas_call(multiply_kernel, grid=(steps,), in_specs=[pl.BlockSpec(mem...  14.6 us
    all_to_all x1, starting transfers between devices, on_device(): sums = lax.all_to_all(sums.transpose(1, 0, 2), 'tm', 0, 0)  9.65 us
    pallas_call x1, Pallas kernels, rescale(): pl.pallas_call(scale_kernel, grid=(total // GROUP,), in_specs=[pl.BlockSp...  7.4 us
    all_to_all x1, starting transfers between devices, on_device(): lax.all_to_all(finish_sums(pairs, sums, late[0, 0, :GROUP, :LANES], frame...  5.68 us
    pallas_call x1, Pallas kernels, cut(): pl.pallas_call(cut_kernel, grid=(1,), in_specs=[pl.BlockSpec((streams, si...  3.01 us
    ppermute x1, starting transfers between devices, shifted(): return lax.ppermute(array, axis, pairs)  2.51 us
    all_to_all x1, waiting for transfers between devices, on_device(): lax.all_to_all(finish_sums(pairs, sums, late[0, 0, :GROUP, :LANES], frame...  2.28 us
  transfers between devices with their start and end apart: 3, of which 2 were waited for; matrix products, arithmetic and copies ran while one was open for 4% of the time, Pallas kernels for 40%

profile of v2, /device:TPU:0, one launch (start us, length us, event | category | flops | bytes accessed | tf_op | source)
XLA Modules:
  0.0 85.0 jit_solution(3988120643464264865)
XLA Ops:
  0.6 0.0 copy-start.3
  0.6 0.0 copy-start.2
  0.6 3.0 %cut.1 = s32[4,960,128]{2,1,0:T(8,128)} custom-call(s32[4,3072,128]{2,1,0:T(8,128)} %bitcast.16, s32[4,3072,128]{2,1,0:T(8,128)} %bitcast.17), custom_call_target="tpu_custom_call" | custom-call | tf_op jit(solution)/shard_map/cut/pallas_call | solution.py:80
  3.7 2.5 %collective-permute-start = (s32[4,960,128]{2,1,0:T(8,128)}, s32[4,960,128]{2,1,0:T(8,128)S(1)}, u32[]{:S(2)}, u32[]{:S(2)}) collective-permute-start(s32[4,960,128]{2,1,0:T(8,128)} %cut.1), channel_id=1, source_target_pairs={{0,1},{1,2},{2,3},{3,4},{4,5},{5,6},{6,7},{7,8},{8,9},{9,10},{10,1... | collective-permute-start | bytes 5898248 | tf_op jit(solution)/shard_map/ppermute | solution.py:19
  6.2 0.0 copy-done.3
  6.2 0.7 copy.19.pairs
  6.9 0.0 copy-done.2
  6.9 0.1 copy.21
  6.9 1.0 %broadcast_in_dim.6 = f32[16,32,2,128]{3,2,1,0:T(2,128)} broadcast(f32[16,32,128]{2,1,0:T(8,128)S(1)} %bitcast.24), dimensions={0,1,3} | broadcast | bytes 786432 | tf_op jit(solution)/shard_map/broadcast_in_dim | solution.py:378
  7.9 0.7 broadcast_in_dim.7.acc_in
  8.6 19.0 %channelize.2 = (f32[4,1024,256]{2,1,0:T(8,128)}, f32[12,32,128]{2,1,0:T(8,128)}) custom-call(s32[4,2]{1,0:T(4,128)} %copy.19.pairs, f32[16,64,128]{2,1,0:T(8,128)} %bitcast.22, bf16[64,256]{1,0:T(8,128)(2,1)} %constant.8.clone.left, f32[2,32,128]{2,1,0:T(8,128)} %constant.9.clone.twist, bf16[768,256]{1,0:T(8,128)(2,1)} %constant.10.clone.right, ...), custom_call_target="tpu_custom_call" | custom-call | tf_op jit(solution)/shard_map/channelize/pallas_call | solution.py:231
  27.6 0.0 collective-permute-done.rest_0_
  27.6 0.0 copy-start.1
  27.6 1.3 %copy-done.1 = s32[4,960,128]{2,1,0:T(8,128)} copy-done((s32[4,960,128]{2,1,0:T(8,128)}, s32[4,960,128]{2,1,0:T(8,128)S(1)}, u32[]{:S(2)}) %copy-start.1) | copy-done | bytes 1966104
  28.9 11.7 %channelize.3 = (f32[4,512,256]{2,1,0:T(8,128)}, f32[12,32,128]{2,1,0:T(8,128)}) custom-call(s32[4,2]{1,0:T(4,128)} %copy.19.pairs, f32[16,64,128]{2,1,0:T(8,128)} %bitcast.23, bf16[64,256]{1,0:T(8,128)(2,1)} %constant.8.clone.left, f32[2,32,128]{2,1,0:T(8,128)} %constant.9.clone.twist, bf16[768,256]{1,0:T(8,128)(2,1)} %constant.10.clone.right, ...), custom_call_target="tpu_custom_call" | custom-call | tf_op jit(solution)/shard_map/channelize/pallas_call | solution.py:231
  40.6 1.0 %reshape.26 = f32[12,16,256]{2,1,0:T(8,128)S(1)} reshape(f32[12,32,128]{2,1,0:T(8,128)} %get-tuple-element.7) | data formatting | bytes 393216 | tf_op jit(solution)/shard_map/reshape | solution.py:383
  41.6 0.8 copy.23
  42.4 9.6 %all-to-all-start = ((f32[16,12,256]{2,1,0:T(8,128)}), f32[16,12,256]{2,1,0:T(8,128)S(1)}, u32[]{:S(2)}, u32[]{:S(2)}) async-start(f32[16,12,256]{2,1,0:T(8,128)} %bitcast.15), calls=%async_computation | async-start | bytes 524288 | tf_op jit(solution)/shard_map/all_to_all | solution.py:384
  52.1 0.0 copy-start
  52.1 9.0 %multiply.2.late = f32[2,4,32,4096]{3,2,1,0:T(8,128)} custom-call(s32[4,2]{1,0:T(4,128)} %copy.19.pairs, f32[4,1024,256]{2,1,0:T(8,128)} %get-tuple-element.8.spec), custom_call_target="tpu_custom_call" | custom-call | tf_op jit(solution)/shard_map/multiply/pallas_call | solution.py:290
  61.1 0.7 slice_bitcast_fusion.after
  61.7 0.3 all-to-all-done.sums
  62.1 0.0 copy-done
  62.1 1.3 %finish.1 = f32[16,8,256]{2,1,0:T(8,128)} custom-call(s32[4,2]{1,0:T(4,128)S(1)} %copy-done, f32[16,12,256]{2,1,0:T(8,128)S(1)} %all-to-all-done.sums, f32[8,128]{1,0:T(8,128)S(1)} %slice_bitcast_fusion.after), custom_call_target="tpu_custom_call" | custom-call | tf_op jit(solution)/shard_map/finish/pallas_call | solution.py:324
  63.4 5.7 %all-to-all-start.1 = ((f32[16,8,256]{2,1,0:T(8,128)}), f32[16,8,256]{2,1,0:T(8,128)S(1)}, u32[]{:S(2)}, u32[]{:S(2)}) async-start(f32[16,8,256]{2,1,0:T(8,128)} %finish.1), calls=%async_computation.1 | async-start | bytes 262144 | tf_op jit(solution)/shard_map/all_to_all | solution.py:386
  69.1 5.6 %multiply.3.early = f32[2,4,16,4096]{3,2,1,0:T(8,128)} custom-call(s32[4,2]{1,0:T(4,128)} %copy.19.pairs, f32[4,512,256]{2,1,0:T(8,128)} %get-tuple-element.9.spec), custom_call_target="tpu_custom_call" | custom-call | tf_op jit(solution)/shard_map/multiply/pallas_call | solution.py:290
  74.7 2.3 %all-to-all-done.1 = f32[16,8,256]{2,1,0:T(8,128)S(1)} async-done(((f32[16,8,256]{2,1,0:T(8,128)}), f32[16,8,256]{2,1,0:T(8,128)S(1)}, u32[]{:S(2)}, u32[]{:S(2)}) %all-to-all-start.1) | async-done | bytes 131104 | tf_op jit(solution)/shard_map/all_to_all | solution.py:386
  77.0 0.7 fusion
  77.6 7.4 %rescale.1 = f32[2,4,48,4096]{3,2,1,0:T(8,128)} custom-call(f32[4,4096]{1,0:T(4,128)} %bitcast.26, f32[2,4,16,4096]{3,2,1,0:T(8,128)} %multiply.3.early, f32[2,4,32,4096]{3,2,1,0:T(8,128)} %multiply.2.late), custom_call_target="tpu_custom_call" | custom-call | tf_op jit(solution)/shard_map/rescale/pallas_call | solution.py:350
Async XLA Ops:
  0.6 5.6 %copy-start.3 = (s32[4,2]{0,1:T(2,128)S(1)}, s32[4,2]{0,1:T(2,128)}, u32[]{:S(2)}) copy-start(s32[4,2]{0,1:T(2,128)} %param.8) | copy-start | bytes 100
  0.6 6.2 %copy-start.2 = (f32[16,4096]{1,0:T(8,128)S(1)}, f32[16,4096]{1,0:T(8,128)}, u32[]{:S(2)}) copy-start(f32[16,4096]{1,0:T(8,128)} %param.7) | copy-start | bytes 786436
  3.7 23.9 %collective-permute-start = (s32[4,960,128]{2,1,0:T(8,128)}, s32[4,960,128]{2,1,0:T(8,128)S(1)}, u32[]{:S(2)}, u32[]{:S(2)}) collective-permute-start(s32[4,960,128]{2,1,0:T(8,128)} %cut.1), channel_id=1, source_target_pairs={{0,1},{1,2},{2,3},{3,4},{4,5},{5,6},{6,7},{7,8},{8,9},{9,10},{10,1... | collective-permute-start | bytes 5898248 | tf_op jit(solution)/shard_map/ppermute | solution.py:19
  27.6 1.3 %copy-start.1 = (s32[4,960,128]{2,1,0:T(8,128)}, s32[4,960,128]{2,1,0:T(8,128)S(1)}, u32[]{:S(2)}) copy-start(s32[4,960,128]{2,1,0:T(8,128)S(1)} %collective-permute-done.rest_0_) | copy-start | bytes 5898244
  42.4 19.7 %all-to-all-start = ((f32[16,12,256]{2,1,0:T(8,128)}), f32[16,12,256]{2,1,0:T(8,128)S(1)}, u32[]{:S(2)}, u32[]{:S(2)}) async-start(f32[16,12,256]{2,1,0:T(8,128)} %bitcast.15), calls=%async_computation | async-start | bytes 524288 | tf_op jit(solution)/shard_map/all_to_all | solution.py:384
  52.1 10.0 %copy-start = (s32[4,2]{1,0:T(4,128)S(1)}, s32[4,2]{1,0:T(4,128)}, u32[]{:S(2)}) copy-start(s32[4,2]{1,0:T(4,128)} %copy.19.pairs) | copy-start | bytes 100
  63.4 13.6 %all-to-all-start.1 = ((f32[16,8,256]{2,1,0:T(8,128)}), f32[16,8,256]{2,1,0:T(8,128)S(1)}, u32[]{:S(2)}, u32[]{:S(2)}) async-start(f32[16,8,256]{2,1,0:T(8,128)} %finish.1), calls=%async_computation.1 | async-start | bytes 262144 | tf_op jit(solution)/shard_map/all_to_all | solution.py:386
